TPU v7x, 32 devices: a whole 2x2x4 slice. The times are simulated.
32 devices in a mesh: head: 4 (over y, x), blk: 8 (over z, core).
Axes of the slice: x: 2, y: 2, z: 4, core: 2. Of those that a mesh axis runs over, the one named last changes fastest.
Arguments:
- hidden_in: bfloat16 [2048, 4096], P(('blk', 'head')), may hold values from -6 to 6
- queries: bfloat16 [2048, 2048], P(('blk', 'head')), may hold values from -26 to 26
- key_states: bfloat16 [2048, 1024], P(('blk', 'head')), may hold values from -5 to 5
- value_states: bfloat16 [2048, 1024], P(('blk', 'head')), may hold values from -6 to 6
- out_weight: bfloat16 [2048, 4096], P('head'), may hold values from -0.125 to 0.125
- norm_gain: float32 [4096], replicated, may hold values from 0.1 to 1.9
- gate_weight: bfloat16 [4096, 7168], P(None, 'head'), may hold values from -0.09375 to 0.09375
- up_weight: bfloat16 [4096, 7168], P(None, 'head'), may hold values from -0.09375 to 0.09375
- down_weight: bfloat16 [7168, 4096], P('head'), may hold values from -0.0625 to 0.0625
Outputs:
- layer_out: bfloat16 [2048, 4096], P(('blk', 'head'))
All inputs are finite; a program needn't handle non-finite values.
Results may differ from a plain program's by a relative error of at most 0.018.
Values may be sent and summed in bfloat16 or wider, within the bound.
A program may use at most 192 MiB of HBM per device.

v0:
```python
import functools

import jax
import jax.numpy as jnp
from jax import lax
from jax.experimental import pallas as pl
from jax.experimental.pallas import tpu as pltpu
from jax.sharding import PartitionSpec as P

HEADS = 16
KV_HEADS = 8
HEAD_DIM = 128
CHUNKS = 4
AHEAD = 2
MESH = pl.DeviceIdType.MESH
BF = jnp.bfloat16
F32 = jnp.float32


def tile_of(n, most=256):
    t = most
    while n % t:
        t -= 128
    return t


def remote(src, dst, send, recv, axis, index):
    return pltpu.make_async_remote_copy(
        src_ref=src, dst_ref=dst, send_sem=send, recv_sem=recv,
        device_id={axis: index}, device_id_type=MESH,
    )


def kernel(
    H, B,
    hid, q_in, k_in, v_in, gain, wo_h, wg_h, wu_h, wd_h,
    out,
    wo, wg, wu, wd, qb, kv, att, part, rs, gath, accg, accu, inner,
    w_sem, loc_sem, a_s, a_r, z_s, z_r, d_s, d_r, rs_s, rs_r, ag_s, ag_r, r2_s, r2_r,
):
    h = lax.axis_index("head")
    b = lax.axis_index("blk")
    J = B // 2
    j = b // 2
    c = b % 2
    partner = b + 1 - 2 * c
    T = hid.shape[0]
    D = hid.shape[1]
    R = T * H
    QW = qb.shape[1]
    KW = kv.shape[3]
    nh = QW // HEAD_DIM
    ratio = HEADS // KV_HEADS
    CW = D // CHUNKS
    FW = wg.shape[1]

    wcopies = [pltpu.make_async_copy(wo_h, wo, w_sem.at[0])]
    for i in range(CHUNKS):
        rows = pl.ds(i * CW, CW)
        wcopies.append(pltpu.make_async_copy(wg_h.at[rows], wg.at[rows], w_sem.at[1 + 2 * i]))
        wcopies.append(pltpu.make_async_copy(wu_h.at[rows], wu.at[rows], w_sem.at[2 + 2 * i]))
    wcopies.append(pltpu.make_async_copy(wd_h, wd, w_sem.at[1 + 2 * CHUNKS]))
    barrier = pltpu.get_barrier_semaphore()
    for d in range(1, H):
        pl.semaphore_signal(barrier, inc=1, device_id={"head": lax.rem(h + d, H)}, device_id_type=MESH)

    @pl.when(j > 0)
    def _():
        pl.semaphore_signal(barrier, inc=1, device_id={"blk": lax.rem(b + B - 2, B)}, device_id_type=MESH)

    @pl.when(j < J - 1)
    def _():
        pl.semaphore_signal(barrier, inc=1, device_id={"blk": lax.rem(b + 2, B)}, device_id_type=MESH)

    pl.semaphore_signal(barrier, inc=1, device_id={"blk": partner}, device_id_type=MESH)
    pl.semaphore_wait(barrier, H + jnp.minimum(j, 1) + jnp.minimum(J - 1 - j, 1))

    my_rows = pl.ds(pl.multiple_of(h * T, T), T)

    def cols(p, w):
        return pl.ds(pl.multiple_of(p * w, w), w)

    a_copies = []
    for t, (src, dst, w) in enumerate(
        ((k_in, kv.at[b, 0], KW), (v_in, kv.at[b, 1], KW), (q_in, qb, QW))
    ):
        for d in range(1, H):
            p = lax.rem(h + d, H)
            cp = remote(
                src.at[:, cols(p, w)], dst.at[my_rows, :],
                a_s.at[d - 1, t], a_r.at[d - 1, t], "head", p,
            )
            cp.start()
            a_copies.append((t, cp))
        lc = pltpu.make_async_copy(src.at[:, cols(h, w)], dst.at[my_rows, :], loc_sem.at[t])
        lc.start()
        a_copies.append((t, lc))

    def wait_in(t):
        for tt, cp in a_copies:
            if tt == t:
                cp.wait()

    def z_copy(slot, t):
        return remote(
            kv.at[slot, t], kv.at[slot, t], z_s.at[slot, t], z_r.at[slot, t],
            "blk", lax.rem(b + 2, B),
        )

    def d_copy(slot, t):
        return remote(
            kv.at[slot, t], kv.at[slot, t], d_s.at[slot, t], d_r.at[slot, t], "blk", partner
        )

    for t in range(2):
        wait_in(t)

        @pl.when(j < J - 1)
        def _():
            z_copy(b, t).start()

        @pl.when(c == 0)
        def _():
            d_copy(b, t).start()

    wait_in(2)
    for w in wcopies:
        w.start()

    mq = lambda n: slice(n * HEAD_DIM, (n + 1) * HEAD_DIM)
    ml = lambda n: slice((nh + n) * HEAD_DIM, (nh + n + 1) * HEAD_DIM)
    scale = HEAD_DIM ** (-0.5)

    def absorb(slot, first):
        for n in range(nh):
            g = n // ratio
            s = lax.dot_general(
                qb[:, mq(n)], kv[slot, 0, :, mq(g)],
                (((1,), (1,)), ((), ())), preferred_element_type=F32,
            ) * scale
            if first:
                qi = lax.broadcasted_iota(jnp.int32, s.shape, 0)
                ki = lax.broadcasted_iota(jnp.int32, s.shape, 1)
                s = jnp.where(ki <= qi, s, -1e30)
            top = jnp.max(s, axis=1, keepdims=True)
            if not first:
                old = accu[:, mq(n)][:, :1]
                top = jnp.maximum(top, old)
            e = jnp.exp(s - top)
            tot = jnp.sum(e, axis=1, keepdims=True)
            pv = jnp.dot(e.astype(BF), kv[slot, 1, :, mq(g)], preferred_element_type=F32)
            if not first:
                f = jnp.exp(old - top)
                tot = tot + accu[:, ml(n)][:, :1] * f
                pv = pv + accg[:, mq(n)] * f
            accu[:, mq(n)] = jnp.broadcast_to(top, (R, HEAD_DIM))
            accu[:, ml(n)] = jnp.broadcast_to(tot, (R, HEAD_DIM))
            accg[:, mq(n)] = pv

    absorb(b, True)

    @pl.when(c == 1)
    def _():
        for t in range(2):
            d_copy(b - 1, t).wait_recv()
        absorb(b - 1, False)

    def chain(s, carry):
        slot = 2 * (j - 1 - s) + c
        other = 2 * (j - 1 - s) + 1 - c
        for t in range(2):
            z_copy(slot, t).wait_recv()

            @pl.when(j < J - 1)
            def _():
                z_copy(slot, t).start()

            d_copy(slot, t).start()
        absorb(slot, False)
        for t in range(2):
            d_copy(other, t).wait_recv()
        absorb(other, False)
        return carry

    lax.fori_loop(0, j, chain, 0)

    for n in range(nh):
        att[:, mq(n)] = (accg[:, mq(n)] / accu[:, ml(n)]).astype(BF)

    square_ring = H == 4
    nx = h + 1 - 2 * (h % 2)
    ny = lax.rem(h + H // 2, H)
    dg = H - 1 - h
    HW = CW // 2

    def rows_of(p):
        return pl.ds(pl.multiple_of(p * T, T), T)

    def halves(i):
        return pl.ds(i * CW, HW), pl.ds(i * CW + HW, HW)

    def scatter(w_ref, x_ref, send, recv):
        copies = {}
        ct = tile_of(CW)
        for i in range(CHUNKS):
            def step(t, carry):
                cs = pl.ds(pl.multiple_of(i * CW + t * ct, ct), ct)
                part[:, cs] = jnp.dot(
                    x_ref[...], w_ref[:, cs], preferred_element_type=F32
                ).astype(BF)
                return carry

            lax.fori_loop(0, CW // ct, step, 0)
            if square_ring:
                ha, hb = halves(i)
                plan = ((1, dg, ha, 0, nx), (1, dg, hb, 1, ny), (0, nx, ha, 2, nx), (0, ny, hb, 3, ny))
            else:
                cs = pl.ds(i * CW, CW)
                plan = [(d - 1, lax.rem(h + d, H), cs, d - 1, lax.rem(h + d, H)) for d in range(1, H)]
            for place, block, cs, sem, to in plan:
                cp = remote(
                    part.at[rows_of(block), cs], rs.at[place, :, cs],
                    send.at[sem, i], recv.at[sem, i], "head", to,
                )
                cp.start()
                copies[sem, i] = cp
        return copies

    def combine(i, copies, send, recv):
        if not square_ring:
            return
        ha, hb = halves(i)
        for cs, sem, to in ((ha, 0, ny), (hb, 1, nx)):
            copies[sem, i].wait_recv()
            blk_rows = rows_of(to)
            part[blk_rows, cs] = (
                part[blk_rows, cs].astype(F32) + rs[1, :, cs].astype(F32)
            ).astype(BF)
            cp = remote(
                part.at[blk_rows, cs], rs.at[2, :, cs],
                send.at[4 + sem, i], recv.at[4 + sem, i], "head", to,
            )
            cp.start()
            copies[4 + sem, i] = cp

    def reduced(i, copies):
        cs = pl.ds(i * CW, CW)
        sems = (2, 3, 4, 5) if square_ring else range(H - 1)
        for sem in sems:
            copies[sem, i].wait_recv()
        total = part[my_rows, cs].astype(F32)
        for place in (0, 2) if square_ring else range(H - 1):
            total = total + rs[place, :, cs].astype(F32)
        return total

    wcopies[0].wait()
    rs_copies = scatter(wo, att, rs_s, rs_r)
    ag_copies = {}

    def spread(rows, cs, sem, i, to):
        cp = remote(
            gath.at[rows, cs], gath.at[rows, cs],
            ag_s.at[sem, i], ag_r.at[sem, i], "head", to,
        )
        cp.start()
        ag_copies[sem, i] = cp

    def spread_own(i):
        for sem, to in enumerate(
            (nx, ny) if square_ring else [lax.rem(h + d, H) for d in range(1, H)]
        ):
            spread(my_rows, pl.ds(i * CW, CW), sem, i, to)

    for i in range(CHUNKS + 1):
        if i < CHUNKS:
            combine(i, rs_copies, rs_s, rs_r)
        if i:
            cs = pl.ds((i - 1) * CW, CW)
            gath[my_rows, cs] = (hid[:, cs].astype(F32) + reduced(i - 1, rs_copies)).astype(BF)
            if i <= AHEAD or not square_ring:
                spread_own(i - 1)

    ft = tile_of(FW)
    square = jnp.zeros((R, 1), F32)
    for i in range(CHUNKS + 1):
        if i < CHUNKS and square_ring:
            ha, hb = halves(i)
            ag_copies[0, i].wait_recv()
            spread(rows_of(nx), ha, 2, i, ny)
            ag_copies[1, i].wait_recv()
            spread(rows_of(ny), hb, 3, i, nx)
            if i + AHEAD < CHUNKS:
                spread_own(i + AHEAD)
        if i == 0:
            continue
        k = i - 1
        cs = pl.ds(k * CW, CW)
        for sem in (2, 3) if square_ring else range(H - 1):
            ag_copies[sem, k].wait_recv()
        wcopies[1 + 2 * k].wait()
        wcopies[2 + 2 * k].wait()
        x = gath[:, cs].astype(F32)
        square = square + jnp.sum(x * x, axis=1, keepdims=True)
        xg = (x * gain[:, cs]).astype(BF)

        def step(t, carry, xg=xg, cs=cs, k=k):
            fs = pl.ds(pl.multiple_of(t * ft, ft), ft)
            g = jnp.dot(xg, wg[cs, fs], preferred_element_type=F32)
            u = jnp.dot(xg, wu[cs, fs], preferred_element_type=F32)
            if k:
                g = g + accg[:, fs]
                u = u + accu[:, fs]
            accg[:, fs] = g
            accu[:, fs] = u
            return carry

        lax.fori_loop(0, FW // ft, step, 0)
    r = lax.rsqrt(square / D + 1e-5)

    def act(t, carry):
        fs = pl.ds(pl.multiple_of(t * ft, ft), ft)
        g = accg[:, fs] * r
        u = accu[:, fs] * r
        inner[:, fs] = (g / (1.0 + jnp.exp(-g)) * u).astype(BF)
        return carry

    lax.fori_loop(0, FW // ft, act, 0)
    for cp in rs_copies.values():
        cp.wait_send()
    wcopies[-1].wait()
    r2_copies = scatter(wd, inner, r2_s, r2_r)
    for i in range(CHUNKS + 1):
        if i < CHUNKS:
            combine(i, r2_copies, r2_s, r2_r)
        if i:
            cs = pl.ds((i - 1) * CW, CW)
            out[:, cs] = (gath[my_rows, cs].astype(F32) + reduced(i - 1, r2_copies)).astype(BF)

    for cp in (*ag_copies.values(), *r2_copies.values()):
        cp.wait_send()
    for t in range(2):
        @pl.when(j < J - 1)
        def _():
            z_copy(b, t).wait_send()

        @pl.when(c == 0)
        def _():
            d_copy(b, t).wait_send()

    def drain(s, carry):
        slot = 2 * (j - 1 - s) + c
        for t in range(2):
            @pl.when(j < J - 1)
            def _():
                z_copy(slot, t).wait_send()

            d_copy(slot, t).wait_send()
        return carry

    lax.fori_loop(0, j, drain, 0)


def solution(mesh):
    H = mesh.shape["head"]
    B = mesh.shape["blk"]

    def local(hid, q, k, v, wo, gain, wg, wu, wd):
        T, D = hid.shape
        R = T * H
        QW = q.shape[1] // H
        KW = k.shape[1] // H
        FW = wg.shape[1]
        vm = pl.BlockSpec(memory_space=pltpu.VMEM)
        hbm = pl.BlockSpec(memory_space=pl.ANY)
        dma = pltpu.SemaphoreType.DMA
        return pl.pallas_call(
            functools.partial(kernel, H, B),
            out_shape=jax.ShapeDtypeStruct((T, D), BF),
            in_specs=[vm] * 5 + [hbm] * 4,
            out_specs=vm,
            scratch_shapes=[
                pltpu.VMEM(wo.shape, BF),
                pltpu.VMEM(wg.shape, BF),
                pltpu.VMEM(wu.shape, BF),
                pltpu.VMEM(wd.shape, BF),
                pltpu.VMEM((R, QW), BF),
                pltpu.VMEM((B, 2, R, KW), BF),
                pltpu.VMEM((R, QW), BF),
                pltpu.VMEM((R, D), BF),
                pltpu.VMEM((H - 1, T, D), BF),
                pltpu.VMEM((R, D), BF),
                pltpu.VMEM((R, FW), F32),
                pltpu.VMEM((R, FW), F32),
                pltpu.VMEM((R, FW), BF),
                dma((2 + 2 * CHUNKS,)),
                dma((3,)),
                dma((H - 1, 3)), dma((H - 1, 3)),
                dma((B, 2)), dma((B, 2)),
                dma((B, 2)), dma((B, 2)),
                dma((max(H - 1, 6), CHUNKS)), dma((max(H - 1, 6), CHUNKS)),
                dma((max(H - 1, 6), CHUNKS)), dma((max(H - 1, 6), CHUNKS)),
                dma((max(H - 1, 6), CHUNKS)), dma((max(H - 1, 6), CHUNKS)),
            ],
            compiler_params=pltpu.CompilerParams(
                collective_id=0, has_side_effects=True, vmem_limit_bytes=67_043_328
            ),
        )(hid, q, k, v, gain.reshape(1, -1), wo, wg, wu, wd)

    rows = P(("blk", "head"), None)
    return jax.shard_map(
        local,
        mesh=mesh,
        in_specs=(rows, rows, rows, rows, P("head", None), P(), P(None, "head"), P(None, "head"), P("head", None)),
        out_specs=rows,
        check_vma=False,
    )
```

profile of v0, /device:TPU:24, one launch (start us, length us, event | category | flops | bytes accessed | tf_op | source)
XLA Modules:
  0.0 99.3 jit_solution(18370081841283751491)
XLA Ops:
  0.0 97.4 %shard_map.91 = bf16[64,4096]{1,0:T(8,128)(2,1)} custom-call(bf16[64,4096]{1,0:T(8,128)(2,1)} %hid.1, bf16[64,2048]{1,0:T(8,128)(2,1)} %q_in.1, bf16[64,1024]{1,0:T(8,128)(2,1)} %k_in.1, bf16[64,1024]{1,0:T(8,128)(2,1)} %v_in.1, f32[1,4096]{1,0:T(1,128)} %bitcast.1, bf16[512,4096]{1,0:T(8,128)(2,1)} %wo_h.1, bf16[4096,1792]{1,0:T(8,128)(2,1)} %wg_h.1, ...), custom_call_target="tpu_custom_call" | custom-call | tf_op jit(solution)/shard_map/pallas_call | solution.py:376
  97.4 1.9 %copy.11 = bf16[64,4096]{1,0:T(8,128)(2,1)} copy(bf16[64,4096]{1,0:T(8,128)(2,1)} %shard_map.91) | data formatting | bytes 1048576
where the time goes:
time: 99.5 us; the launch traced here: 99.3 us
  Pallas kernels  97.4 us (98%)
  local copies, waits for them, and re-layouts  1.87 us (2%)
    pallas_call x1, Pallas kernels, local(): pl.pallas_call(functools.partial(kernel, H, B), out_shape=jax.ShapeDtypeS...  97.4 us

commit v1 on v0

--- a/solution.py
+++ b/solution.py
@@ -12,6 +12,10 @@
 HEAD_DIM = 128
 CHUNKS = 4
 AHEAD = 2
+SUBS = 4
+LEAD = 4
+RCHUNKS = 8
+LOG2E = 1.4426950408889634
 MESH = pl.DeviceIdType.MESH
 BF = jnp.bfloat16
 F32 = jnp.float32
@@ -31,7 +35,7 @@
     )
 
 
-def kernel(
+def general_kernel(
     H, B,
     hid, q_in, k_in, v_in, gain, wo_h, wg_h, wu_h, wd_h,
     out,
@@ -360,11 +364,463 @@
     lax.fori_loop(0, j, drain, 0)
 
 
+def square_kernel(
+    H, B,
+    hid, q_in, k_in, v_in, gain, wo_h, wg_h, wu_h, wd_h,
+    out,
+    wo, wg, wu, wd, qb, kv, att, attx, hx, sb, rb, part, rs, gath, accg, accu, inner,
+    w_sem, a_s, a_r, z_s, z_r, d_s, d_r, x_s, x_r, at_s, at_r, o_s, o_r, ag_s, ag_r, r2_s, r2_r,
+):
+    h = lax.axis_index("head")
+    b = lax.axis_index("blk")
+    J = B // 2
+    j = b // 2
+    c = b % 2
+    partner = b + 1 - 2 * c
+    T, D = hid.shape
+    R = T * H
+    G, QR = qb.shape[0], qb.shape[1]
+    ratio = QR // R
+    QW = att.shape[1]
+    GW = QW // G
+    FW = wg.shape[1]
+    half = D // 2
+    DW = D // 4
+    SW = DW // SUBS
+    CW = D // RCHUNKS
+
+    ex, ey = h % 2, h // 2
+    nx = h + 1 - 2 * ex
+    ny = lax.rem(h + 2, H)
+    dg = H - 1 - h
+    pair = (nx, ny)
+    across = (ny, nx)
+    mine = (ex, ey)
+
+    wcopies = []
+    for s in range(2):
+        src = wo_h.at[:, pl.ds(pl.multiple_of(s * half + mine[s] * DW, DW), DW)]
+        wcopies.append((src, wo.at[s, pl.ds(0, QW)]))
+    for i in range(CHUNKS):
+        rows = pl.ds(i * (D // CHUNKS), D // CHUNKS)
+        wcopies.append((wg_h.at[rows], wg.at[rows]))
+        wcopies.append((wu_h.at[rows], wu.at[rows]))
+    wcopies.append((wd_h, wd))
+    wcopies = [pltpu.make_async_copy(s, d, w_sem.at[n]) for n, (s, d) in enumerate(wcopies)]
+
+    barrier = pltpu.get_barrier_semaphore()
+    for d in range(1, H):
+        pl.semaphore_signal(barrier, inc=1, device_id={"head": lax.rem(h + d, H)}, device_id_type=MESH)
+
+    @pl.when(j > 0)
+    def _():
+        pl.semaphore_signal(barrier, inc=1, device_id={"blk": lax.rem(b + B - 2, B)}, device_id_type=MESH)
+
+    @pl.when(j < J - 1)
+    def _():
+        pl.semaphore_signal(barrier, inc=1, device_id={"blk": lax.rem(b + 2, B)}, device_id_type=MESH)
+
+    pl.semaphore_signal(barrier, inc=1, device_id={"blk": partner}, device_id_type=MESH)
+    pl.semaphore_wait(barrier, H + jnp.minimum(j, 1) + jnp.minimum(J - 1 - j, 1))
+
+    def rows_of(p):
+        return pl.ds(pl.multiple_of(p * T, T), T)
+
+    my_rows = rows_of(h)
+
+    def head_cols(n):
+        return pl.ds(pl.multiple_of(n * HEAD_DIM, HEAD_DIM), HEAD_DIM)
+
+    def q_rows(r, p):
+        return pl.ds(pl.multiple_of(r * R + p * T, T), T)
+
+    pieces = []
+    for g in range(G):
+        pieces.append((k_in, G, g, lambda p, g=g: kv.at[b, g, 0, rows_of(p), :]))
+        pieces.append((v_in, G, g, lambda p, g=g: kv.at[b, g, 1, rows_of(p), :]))
+    for n in range(G * ratio):
+        pieces.append((q_in, G * ratio, n, lambda p, n=n: qb.at[n // ratio, q_rows(n % ratio, p), :]))
+    a_copies = []
+    for t, (src, per, n, dst) in enumerate(pieces):
+        cps = []
+        for d, p in enumerate((dg, nx, ny)):
+            cp = remote(src.at[:, head_cols(p * per + n)], dst(h), a_s.at[d, t], a_r.at[d, t], "head", p)
+            cp.start()
+            cps.append(cp)
+        a_copies.append(cps)
+
+    x_copies = []
+    for s in range(2):
+        cs = pl.ds(pl.multiple_of(s * half + (1 - mine[s]) * DW, DW), DW)
+        x_copies.append(remote(hid.at[:, cs], hx.at[s], x_s.at[s], x_r.at[s], "head", pair[s]))
+    core_cols = pl.ds(pl.multiple_of(c * (DW // 2), DW // 2), DW // 2)
+    for s in range(2):
+        cs = pl.ds(pl.multiple_of(s * half + (1 - mine[s]) * DW + c * (DW // 2), DW // 2), DW // 2)
+        x_copies.append(remote(
+            wo_h.at[:, cs], wo.at[s, pl.ds(QW, QW), core_cols],
+            x_s.at[2 + s], x_r.at[2 + s], "head", pair[s],
+        ))
+    for cp in x_copies:
+        cp.start()
+    share = []
+    for s in range(2):
+        ref = wo.at[s, pl.ds(QW, QW), core_cols]
+        share.append(remote(ref, ref, x_s.at[4 + s], x_r.at[4 + s], "blk", partner))
+
+    for t, (src, per, n, dst) in enumerate(pieces):
+        dst(h)[...] = src[:, head_cols(h * per + n)]
+
+    def wait_in(t):
+        for cp in a_copies[t]:
+            cp.wait_recv()
+
+    def z_copy(slot, g, t):
+        ref = kv.at[slot, g, t]
+        return remote(ref, ref, z_s.at[slot, g, t], z_r.at[slot, g, t], "blk", lax.rem(b + 2, B))
+
+    def d_copy(slot, g, t):
+        ref = kv.at[slot, g, t]
+        return remote(ref, ref, d_s.at[slot, g, t], d_r.at[slot, g, t], "blk", partner)
+
+    own = [(g, t) for g in range(G) for t in range(2)]
+    for n, (g, t) in enumerate(own):
+        wait_in(n)
+
+        @pl.when((j < J - 1) & ((j == 0) | (n < len(own) - 1)))
+        def _():
+            z_copy(b, g, t).start()
+
+        @pl.when(c == 0)
+        def _():
+            d_copy(b, g, t).start()
+
+    def pass_on(slot, g, t):
+        z_copy(slot, g, t).wait_recv()
+
+        @pl.when(j < J - 1)
+        def _():
+            z_copy(slot, g, t).start()
+
+        d_copy(slot, g, t).start()
+
+    def arrive(s, g):
+        slot = 2 * (j - 1 - s) + c
+        other = 2 * (j - 1 - s) + 1 - c
+        for t in range(2):
+            pass_on(slot, g, t)
+        if g == 0:
+            @pl.when((s == 0) & (j < J - 1))
+            def _():
+                z_copy(b, *own[-1]).start()
+        for t in range(2):
+            d_copy(other, g, t).wait_recv()
+        return slot, other
+
+    for n in range(G * ratio):
+        wait_in(len(own) + n)
+    for w in wcopies:
+        w.start()
+
+    factor = HEAD_DIM ** (-0.5) * LOG2E
+
+    def absorb(g, slots, first):
+        for r in range(ratio):
+            qh = qb[g, r * R:(r + 1) * R, :]
+            scores = []
+            n = g * ratio + r
+            tops = slice(n * HEAD_DIM, (n + 1) * HEAD_DIM)
+            sums = slice(2 * n * HEAD_DIM, 2 * (n + 1) * HEAD_DIM)
+            for slot in slots:
+                sc = lax.dot_general(
+                    qh, kv[slot, g, 0], (((1,), (1,)), ((), ())), preferred_element_type=F32,
+                )
+                if first:
+                    qi = lax.broadcasted_iota(jnp.int32, sc.shape, 0)
+                    ki = lax.broadcasted_iota(jnp.int32, sc.shape, 1)
+                    sc = jnp.where(ki <= qi, sc, -1e30)
+                scores.append(sc)
+            top = jnp.max(scores[0], axis=1, keepdims=True)
+            for sc in scores[1:]:
+                top = jnp.maximum(top, jnp.max(sc, axis=1, keepdims=True))
+            if not first:
+                old = accu[:, tops][:, :1]
+                top = jnp.maximum(top, old)
+            pv = None
+            for sc, slot in zip(scores, slots):
+                e = jnp.exp2((sc - top) * factor).astype(BF)
+                v = kv[slot, g, 1]
+                term = jnp.dot(
+                    e, jnp.concatenate([v, jnp.ones_like(v)], axis=1), preferred_element_type=F32
+                )
+                pv = term if pv is None else pv + term
+            if not first:
+                pv = pv + accg[:, sums] * jnp.exp2((old - top) * factor)
+            accu[:, tops] = jnp.broadcast_to(top, (R, HEAD_DIM))
+            accg[:, sums] = pv
+
+    at_copies = []
+    for g in range(G):
+        absorb(g, (b,), True)
+
+        @pl.when(c == 1)
+        def _(g=g):
+            for t in range(2):
+                d_copy(b - 1, g, t).wait_recv()
+            absorb(g, (b - 1,), False)
+
+        def chain(s, carry, g=g):
+            absorb(g, arrive(s, g), False)
+            return carry
+
+        lax.fori_loop(0, j, chain, 0)
+        for r in range(ratio):
+            n = g * ratio + r
+            pv = accg[:, 2 * n * HEAD_DIM:2 * (n + 1) * HEAD_DIM]
+            att[:, n * HEAD_DIM:(n + 1) * HEAD_DIM] = (pv[:, :HEAD_DIM] / pv[:, HEAD_DIM:]).astype(BF)
+        cs = pl.ds(g * GW, GW)
+        for s in range(2):
+            cp = remote(att.at[:, cs], attx.at[s, :, cs], at_s.at[g, s], at_r.at[g, s], "head", pair[s])
+            cp.start()
+            at_copies.append(cp)
+
+    accs = (accg, accu)
+    for s in range(2):
+        x_copies[2 + s].wait_recv()
+        share[s].start()
+    for s in range(2):
+        wcopies[s].wait()
+        tile = tile_of(DW)
+
+        def own_part(t, carry, s=s):
+            cs = pl.ds(pl.multiple_of(t * tile, tile), tile)
+            accs[s][:, cs] = jnp.dot(att[...], wo[s, :QW, cs], preferred_element_type=F32)
+            return carry
+
+        lax.fori_loop(0, DW // tile, own_part, 0)
+    for s in range(2):
+        share[s].wait_recv()
+    for cp in at_copies:
+        cp.wait_recv()
+
+    co = ({"h": nx, "x": h, "y": dg, "d": ny}, {"h": ny, "x": dg, "y": h, "d": nx})
+    order = [(s, i) for i in range(SUBS) for s in range(2)]
+    o_copies = {}
+    for s, i in order:
+        cs = pl.ds(i * SW, SW)
+        accs[s][:, cs] += jnp.dot(attx[s], wo[s, QW:, i * SW:(i + 1) * SW], preferred_element_type=F32)
+        to = across[s]
+        away = (to, co[s]["y" if s == 0 else "x"])
+        for n, p in enumerate(away):
+            sb[s, n * T:(n + 1) * T, i * SW:(i + 1) * SW] = accs[s][rows_of(p), cs].astype(BF)
+        cp = remote(sb.at[s, :, cs], rb.at[s, :, cs], o_s.at[s, i], o_r.at[s, i], "head", to)
+        cp.start()
+        o_copies[s, i] = cp
+
+    def cols_of(s, i, other):
+        part_index = 1 - mine[s] if other else mine[s]
+        return pl.ds(pl.multiple_of(s * half + part_index * DW + i * SW, SW), SW)
+
+    ag_copies = {}
+
+    def spread(s, i, kind, rows, cs, to):
+        ref = gath.at[rows, cs]
+        cp = remote(ref, ref, ag_s.at[s, i, kind], ag_r.at[s, i, kind], "head", to)
+        cp.start()
+        ag_copies[s, i, kind] = cp
+
+    def spread_own(s, i):
+        cs = cols_of(s, i, False)
+        for n, to in enumerate((nx, ny)):
+            spread(s, i, 2 * n, my_rows, cs, to)
+            spread(s, i, 2 * n + 1, rows_of(co[s]["h"]), cs, to)
+
+    def relay(s, i):
+        ag_copies[s, i, 0].wait_recv()
+        spread(s, i, 4, rows_of(nx), cols_of(s, i, s == 0), ny)
+        ag_copies[s, i, 3].wait_recv()
+        spread(s, i, 5, rows_of(co[s]["y"]), cols_of(s, i, s == 1), nx)
+
+    for s in range(2):
+        x_copies[s].wait_recv()
+    for k, (s, i) in enumerate(order):
+        o_copies[s, i].wait_recv()
+        cs = cols_of(s, i, False)
+        lc = slice(i * SW, (i + 1) * SW)
+        gath[my_rows, cs] = (
+            hid[:, cs].astype(F32) + (accs[s][my_rows, lc] + rb[s, :T, lc].astype(F32))
+        ).astype(BF)
+        cr = rows_of(co[s]["h"])
+        gath[cr, cs] = (
+            hx[s, :, lc].astype(F32) + (accs[s][cr, lc] + rb[s, T:, lc].astype(F32))
+        ).astype(BF)
+        if k < LEAD:
+            spread_own(s, i)
+
+    for w in wcopies[2:-1]:
+        w.wait()
+    ft = tile_of(FW)
+    square = jnp.zeros((R, 1), F32)
+    for k in range(len(order) + 1):
+        if k < len(order):
+            relay(*order[k])
+            if k + LEAD < len(order):
+                spread_own(*order[k + LEAD])
+        if k == 0:
+            continue
+        s, i = order[k - 1]
+        for kind in (1, 2, 4, 5):
+            ag_copies[s, i, kind].wait_recv()
+        at = (s * half + i * SW, s * half + DW + i * SW)
+        xs = []
+        for a in at:
+            x = gath[:, a:a + SW].astype(F32)
+            square = square + jnp.sum(x * x, axis=1, keepdims=True)
+            xs.append((x * gain[:, a:a + SW]).astype(BF))
+
+        def step(t, carry, xs=xs, at=at, k=k):
+            fs = pl.ds(pl.multiple_of(t * ft, ft), ft)
+            for acc, w in ((accg, wg), (accu, wu)):
+                y = jnp.dot(xs[0], w[at[0]:at[0] + SW, fs], preferred_element_type=F32)
+                y = y + jnp.dot(xs[1], w[at[1]:at[1] + SW, fs], preferred_element_type=F32)
+                acc[:, fs] = y + acc[:, fs] if k > 1 else y
+            return carry
+
+        lax.fori_loop(0, FW // ft, step, 0)
+    r = lax.rsqrt(square / D + 1e-5)
+
+    def act(t, carry):
+        fs = pl.ds(pl.multiple_of(t * ft, ft), ft)
+        g = accg[:, fs] * r
+        u = accu[:, fs] * r
+        inner[:, fs] = (g / (1.0 + jnp.exp(-g)) * u).astype(BF)
+        return carry
+
+    lax.fori_loop(0, FW // ft, act, 0)
+    wcopies[-1].wait()
+
+    HW = CW // 2
+
+    def halves(i):
+        return pl.ds(i * CW, HW), pl.ds(i * CW + HW, HW)
+
+    copies = {}
+
+    def send(i, sem, rows, place, cs, to):
+        cp = remote(part.at[rows, cs], rs.at[place, :, cs], r2_s.at[sem, i], r2_r.at[sem, i], "head", to)
+        cp.start()
+        copies[sem, i] = cp
+
+    ct = tile_of(CW)
+    for i in range(RCHUNKS):
+        for t in range(CW // ct):
+            cs = slice(i * CW + t * ct, i * CW + (t + 1) * ct)
+            part[:, cs] = jnp.dot(inner[...], wd[:, cs], preferred_element_type=F32).astype(BF)
+        ha, hb = halves(i)
+        send(i, 0, rows_of(dg), 1, ha, nx)
+        send(i, 1, rows_of(dg), 1, hb, ny)
+        send(i, 2, rows_of(nx), 0, ha, nx)
+        send(i, 3, rows_of(ny), 0, hb, ny)
+    for i in range(RCHUNKS + 1):
+        if i < RCHUNKS:
+            ha, hb = halves(i)
+            for cs, sem, to in ((ha, 0, ny), (hb, 1, nx)):
+                copies[sem, i].wait_recv()
+                rows = rows_of(to)
+                part[rows, cs] = (part[rows, cs].astype(F32) + rs[1, :, cs].astype(F32)).astype(BF)
+                send(i, 4 + sem, rows, 2, cs, to)
+        if i:
+            cs = pl.ds((i - 1) * CW, CW)
+            for sem in (2, 3, 4, 5):
+                copies[sem, i - 1].wait_recv()
+            total = part[my_rows, cs].astype(F32)
+            for place in (0, 2):
+                total = total + rs[place, :, cs].astype(F32)
+            out[:, cs] = (gath[my_rows, cs].astype(F32) + total).astype(BF)
+
+    for cps in a_copies:
+        for cp in cps:
+            cp.wait_send()
+    for cp in (*x_copies, *share, *at_copies, *o_copies.values(), *ag_copies.values(), *copies.values()):
+        cp.wait_send()
+    for g, t in own:
+        @pl.when(j < J - 1)
+        def _():
+            z_copy(b, g, t).wait_send()
+
+        @pl.when(c == 0)
+        def _():
+            d_copy(b, g, t).wait_send()
+
+    def drain(s, carry):
+        slot = 2 * (j - 1 - s) + c
+        for g, t in own:
+            @pl.when(j < J - 1)
+            def _():
+                z_copy(slot, g, t).wait_send()
+
+            d_copy(slot, g, t).wait_send()
+        return carry
+
+    lax.fori_loop(0, j, drain, 0)
+
+
+def square_call(H, B, hid, q, k, v, wo, gain, wg, wu, wd):
+    T, D = hid.shape
+    R = T * H
+    QW = q.shape[1] // H
+    G = k.shape[1] // H // HEAD_DIM
+    FW = wg.shape[1]
+    ratio = QW // HEAD_DIM // G
+    AW = max(FW, D // 4, 2 * QW)
+    vm = pl.BlockSpec(memory_space=pltpu.VMEM)
+    hbm = pl.BlockSpec(memory_space=pl.ANY)
+    dma = pltpu.SemaphoreType.DMA
+    return pl.pallas_call(
+        functools.partial(square_kernel, H, B),
+        out_shape=jax.ShapeDtypeStruct((T, D), BF),
+        in_specs=[vm] * 5 + [hbm] * 4,
+        out_specs=vm,
+        scratch_shapes=[
+            pltpu.VMEM((2, 2 * QW, D // 4), BF),
+            pltpu.VMEM(wg.shape, BF),
+            pltpu.VMEM(wu.shape, BF),
+            pltpu.VMEM(wd.shape, BF),
+            pltpu.VMEM((G, ratio * R, HEAD_DIM), BF),
+            pltpu.VMEM((B, G, 2, R, HEAD_DIM), BF),
+            pltpu.VMEM((R, QW), BF),
+            pltpu.VMEM((2, R, QW), BF),
+            pltpu.VMEM((2, T, D // 4), BF),
+            pltpu.VMEM((2, 2 * T, D // 4), BF),
+            pltpu.VMEM((2, 2 * T, D // 4), BF),
+            pltpu.VMEM((R, D), BF),
+            pltpu.VMEM((3, T, D), BF),
+            pltpu.VMEM((R, D), BF),
+            pltpu.VMEM((R, AW), F32),
+            pltpu.VMEM((R, AW), F32),
+            pltpu.VMEM((R, FW), BF),
+            dma((3 + 2 * CHUNKS,)),
+            dma((H - 1, G * (2 + ratio))), dma((H - 1, G * (2 + ratio))),
+            dma((B, G, 2)), dma((B, G, 2)),
+            dma((B, G, 2)), dma((B, G, 2)),
+            dma((6,)), dma((6,)),
+            dma((G, 2)), dma((G, 2)),
+            dma((2, SUBS)), dma((2, SUBS)),
+            dma((2, SUBS, 6)), dma((2, SUBS, 6)),
+            dma((6, RCHUNKS)), dma((6, RCHUNKS)),
+        ],
+        compiler_params=pltpu.CompilerParams(
+            collective_id=0, has_side_effects=True, vmem_limit_bytes=67_043_328
+        ),
+    )(hid, q, k, v, gain.reshape(1, -1), wo, wg, wu, wd)
+
+
 def solution(mesh):
     H = mesh.shape["head"]
     B = mesh.shape["blk"]
 
     def local(hid, q, k, v, wo, gain, wg, wu, wd):
+        if H == 4:
+            return square_call(H, B, hid, q, k, v, wo, gain, wg, wu, wd)
         T, D = hid.shape
         R = T * H
         QW = q.shape[1] // H
@@ -374,7 +830,7 @@
         hbm = pl.BlockSpec(memory_space=pl.ANY)
         dma = pltpu.SemaphoreType.DMA
         return pl.pallas_call(
-            functools.partial(kernel, H, B),
+            functools.partial(general_kernel, H, B),
             out_shape=jax.ShapeDtypeStruct((T, D), BF),
             in_specs=[vm] * 5 + [hbm] * 4,
             out_specs=vm,

time: 99.5 us -> 97.3 us (0.978)
  Pallas kernels: 97.4 us -> 95.3 us
    pallas_call x1, Pallas kernels: 97.4 us -> 95.3 us  [square_call(): pl.pallas_call(functools.partial(square_kernel, H, B), out_shape=jax.Shap...]
where the time goes in v1:
time: 97.3 us; the launch traced here: 97.1 us
  Pallas kernels  95.3 us (98%)
  local copies, waits for them, and re-layouts  1.87 us (2%)
    pallas_call x1, Pallas kernels, square_call(): pl.pallas_call(functools.partial(square_kernel, H, B), out_shape=jax.Shap...  95.3 us

profile of v1, /device:TPU:24, one launch (start us, length us, event | category | flops | bytes accessed | tf_op | source)
XLA Modules:
  0.0 97.1 jit_solution(7174144436534134428)
XLA Ops:
  0.0 95.3 %shard_map.91 = bf16[64,4096]{1,0:T(8,128)(2,1)} custom-call(bf16[64,4096]{1,0:T(8,128)(2,1)} %hid.1, bf16[64,2048]{1,0:T(8,128)(2,1)} %q_in.1, bf16[64,1024]{1,0:T(8,128)(2,1)} %k_in.1, bf16[64,1024]{1,0:T(8,128)(2,1)} %v_in.1, f32[1,4096]{1,0:T(1,128)} %bitcast.1, bf16[512,4096]{1,0:T(8,128)(2,1)} %wo_h.1, bf16[4096,1792]{1,0:T(8,128)(2,1)} %wg_h.1, ...), custom_call_target="tpu_custom_call" | custom-call | tf_op jit(solution)/shard_map/pallas_call | solution.py:778
  95.3 1.9 %copy.11 = bf16[64,4096]{1,0:T(8,128)(2,1)} copy(bf16[64,4096]{1,0:T(8,128)(2,1)} %shard_map.91) | data formatting | bytes 1048576

commit v2 on v1

--- a/solution.py
+++ b/solution.py
@@ -13,8 +13,10 @@
 CHUNKS = 4
 AHEAD = 2
 SUBS = 4
-LEAD = 4
-RCHUNKS = 8
+LEAD = 3
+LAG = 3
+QB = 128
+WIDTHS = (1, 1, 2, 2, 2)
 LOG2E = 1.4426950408889634
 MESH = pl.DeviceIdType.MESH
 BF = jnp.bfloat16
@@ -379,15 +381,14 @@
     partner = b + 1 - 2 * c
     T, D = hid.shape
     R = T * H
-    G, QR = qb.shape[0], qb.shape[1]
-    ratio = QR // R
-    QW = att.shape[1]
+    G = kv.shape[1]
+    QW = qb.shape[1]
+    ratio = QW // G // HEAD_DIM
     GW = QW // G
     FW = wg.shape[1]
     half = D // 2
     DW = D // 4
     SW = DW // SUBS
-    CW = D // RCHUNKS
 
     ex, ey = h % 2, h // 2
     nx = h + 1 - 2 * ex
@@ -428,23 +429,21 @@
 
     my_rows = rows_of(h)
 
-    def head_cols(n):
-        return pl.ds(pl.multiple_of(n * HEAD_DIM, HEAD_DIM), HEAD_DIM)
-
-    def q_rows(r, p):
-        return pl.ds(pl.multiple_of(r * R + p * T, T), T)
-
     pieces = []
     for g in range(G):
-        pieces.append((k_in, G, g, lambda p, g=g: kv.at[b, g, 0, rows_of(p), :]))
-        pieces.append((v_in, G, g, lambda p, g=g: kv.at[b, g, 1, rows_of(p), :]))
-    for n in range(G * ratio):
-        pieces.append((q_in, G * ratio, n, lambda p, n=n: qb.at[n // ratio, q_rows(n % ratio, p), :]))
+        pieces.append((k_in, G, g, kv.at[b, g, 0, my_rows, :]))
+        pieces.append((v_in, G, g, kv.at[b, g, 1, my_rows, :]))
+    pieces.append((q_in, 1, 0, qb.at[my_rows, :]))
+
+    def piece_cols(p, per, n, dst):
+        w = dst.shape[1]
+        return pl.ds(pl.multiple_of((p * per + n) * w, w), w)
+
     a_copies = []
     for t, (src, per, n, dst) in enumerate(pieces):
         cps = []
         for d, p in enumerate((dg, nx, ny)):
-            cp = remote(src.at[:, head_cols(p * per + n)], dst(h), a_s.at[d, t], a_r.at[d, t], "head", p)
+            cp = remote(src.at[:, piece_cols(p, per, n, dst)], dst, a_s.at[d, t], a_r.at[d, t], "head", p)
             cp.start()
             cps.append(cp)
         a_copies.append(cps)
@@ -468,7 +467,7 @@
         share.append(remote(ref, ref, x_s.at[4 + s], x_r.at[4 + s], "blk", partner))
 
     for t, (src, per, n, dst) in enumerate(pieces):
-        dst(h)[...] = src[:, head_cols(h * per + n)]
+        dst[...] = src[:, piece_cols(h, per, n, dst)]
 
     def wait_in(t):
         for cp in a_copies[t]:
@@ -503,76 +502,93 @@
 
         d_copy(slot, g, t).start()
 
-    def arrive(s, g):
-        slot = 2 * (j - 1 - s) + c
-        other = 2 * (j - 1 - s) + 1 - c
-        for t in range(2):
-            pass_on(slot, g, t)
-        if g == 0:
-            @pl.when((s == 0) & (j < J - 1))
-            def _():
-                z_copy(b, *own[-1]).start()
-        for t in range(2):
-            d_copy(other, g, t).wait_recv()
-        return slot, other
-
-    for n in range(G * ratio):
-        wait_in(len(own) + n)
+    def both(s):
+        first = 2 * (j - 1 - s)
+        return first + c, first + 1 - c
+
+    def pass_on_first(g):
+        @pl.when(j > 0)
+        def _():
+            for t in range(2):
+                pass_on(both(0)[0], g, t)
+
+    pass_on_first(0)
+
+    @pl.when((j > 0) & (j < J - 1))
+    def _():
+        z_copy(b, *own[-1]).start()
+
+    wait_in(len(own))
     for w in wcopies:
         w.start()
 
     factor = HEAD_DIM ** (-0.5) * LOG2E
 
     def absorb(g, slots, first):
+        ones = jnp.ones((R, HEAD_DIM), BF)
+        keys = jnp.concatenate([kv[slot, g, 0] for slot in slots], axis=0)
+        values = jnp.concatenate(
+            [jnp.concatenate([kv[slot, g, 1], ones], axis=1) for slot in slots], axis=0
+        )
         for r in range(ratio):
-            qh = qb[g, r * R:(r + 1) * R, :]
-            scores = []
             n = g * ratio + r
             tops = slice(n * HEAD_DIM, (n + 1) * HEAD_DIM)
             sums = slice(2 * n * HEAD_DIM, 2 * (n + 1) * HEAD_DIM)
-            for slot in slots:
+            for q0 in range(0, R, QB):
+                rows = slice(q0, q0 + QB)
                 sc = lax.dot_general(
-                    qh, kv[slot, g, 0], (((1,), (1,)), ((), ())), preferred_element_type=F32,
+                    qb[rows, tops], keys,
+                    (((1,), (1,)), ((), ())), preferred_element_type=F32,
                 )
+                tiles = [sc[:, t:t + HEAD_DIM] for t in range(0, len(slots) * R, HEAD_DIM)]
                 if first:
-                    qi = lax.broadcasted_iota(jnp.int32, sc.shape, 0)
-                    ki = lax.broadcasted_iota(jnp.int32, sc.shape, 1)
-                    sc = jnp.where(ki <= qi, sc, -1e30)
-                scores.append(sc)
-            top = jnp.max(scores[0], axis=1, keepdims=True)
-            for sc in scores[1:]:
-                top = jnp.maximum(top, jnp.max(sc, axis=1, keepdims=True))
-            if not first:
-                old = accu[:, tops][:, :1]
-                top = jnp.maximum(top, old)
-            pv = None
-            for sc, slot in zip(scores, slots):
-                e = jnp.exp2((sc - top) * factor).astype(BF)
-                v = kv[slot, g, 1]
-                term = jnp.dot(
-                    e, jnp.concatenate([v, jnp.ones_like(v)], axis=1), preferred_element_type=F32
-                )
-                pv = term if pv is None else pv + term
-            if not first:
-                pv = pv + accg[:, sums] * jnp.exp2((old - top) * factor)
-            accu[:, tops] = jnp.broadcast_to(top, (R, HEAD_DIM))
-            accg[:, sums] = pv
-
-    at_copies = []
+                    qi = q0 + lax.broadcasted_iota(jnp.int32, tiles[0].shape, 0)
+                    ki = lax.broadcasted_iota(jnp.int32, tiles[0].shape, 1)
+                    for t in range(R // HEAD_DIM):
+                        tiles[t] = jnp.where(ki + t * HEAD_DIM <= qi, tiles[t], -1e30)
+                top = functools.reduce(jnp.maximum, tiles)
+                top = jnp.broadcast_to(jnp.max(top, axis=1, keepdims=True), top.shape)
+                if not first:
+                    old = accu[rows, tops]
+                    top = jnp.maximum(top, old)
+                peak = top * factor
+                e = jnp.concatenate([jnp.exp2(t * factor - peak).astype(BF) for t in tiles], axis=1)
+                pv = jnp.dot(e, values, preferred_element_type=F32)
+                if not first:
+                    f = jnp.exp2(old * factor - peak)
+                    pv = pv + accg[rows, sums] * jnp.concatenate([f, f], axis=1)
+                accu[rows, tops] = top
+                accg[rows, sums] = pv
+
     for g in range(G):
-        absorb(g, (b,), True)
+        @pl.when(c == 0)
+        def _(g=g):
+            absorb(g, (b,), True)
 
         @pl.when(c == 1)
         def _(g=g):
             for t in range(2):
                 d_copy(b - 1, g, t).wait_recv()
-            absorb(g, (b - 1,), False)
-
+            absorb(g, (b, b - 1), True)
+
+    at_copies = []
+    for g in range(G):
         def chain(s, carry, g=g):
-            absorb(g, arrive(s, g), False)
+            slot, other = both(s)
+
+            @pl.when(s > 0)
+            def _():
+                for t in range(2):
+                    pass_on(slot, g, t)
+
+            for t in range(2):
+                d_copy(other, g, t).wait_recv()
+            absorb(g, (slot, other), False)
             return carry
 
         lax.fori_loop(0, j, chain, 0)
+        if g + 1 < G:
+            pass_on_first(g + 1)
         for r in range(ratio):
             n = g * ratio + r
             pv = accg[:, 2 * n * HEAD_DIM:2 * (n + 1) * HEAD_DIM]
@@ -589,14 +605,9 @@
         share[s].start()
     for s in range(2):
         wcopies[s].wait()
-        tile = tile_of(DW)
-
-        def own_part(t, carry, s=s):
-            cs = pl.ds(pl.multiple_of(t * tile, tile), tile)
+        for t in range(SUBS):
+            cs = slice(t * SW, (t + 1) * SW)
             accs[s][:, cs] = jnp.dot(att[...], wo[s, :QW, cs], preferred_element_type=F32)
-            return carry
-
-        lax.fori_loop(0, DW // tile, own_part, 0)
     for s in range(2):
         share[s].wait_recv()
     for cp in at_copies:
@@ -660,14 +671,15 @@
         w.wait()
     ft = tile_of(FW)
     square = jnp.zeros((R, 1), F32)
-    for k in range(len(order) + 1):
-        if k < len(order):
-            relay(*order[k])
-            if k + LEAD < len(order):
-                spread_own(*order[k + LEAD])
-        if k == 0:
+    for n in range(len(order) + LAG):
+        if n < len(order):
+            relay(*order[n])
+            if n + LEAD < len(order):
+                spread_own(*order[n + LEAD])
+        if n < LAG:
             continue
-        s, i = order[k - 1]
+        k = n - LAG
+        s, i = order[k]
         for kind in (1, 2, 4, 5):
             ag_copies[s, i, kind].wait_recv()
         at = (s * half + i * SW, s * half + DW + i * SW)
@@ -677,31 +689,32 @@
             square = square + jnp.sum(x * x, axis=1, keepdims=True)
             xs.append((x * gain[:, a:a + SW]).astype(BF))
 
-        def step(t, carry, xs=xs, at=at, k=k):
-            fs = pl.ds(pl.multiple_of(t * ft, ft), ft)
+        last = k == len(order) - 1
+        if last:
+            r = lax.rsqrt(square / D + 1e-5)
+        for t in range(FW // ft):
+            fs = slice(t * ft, (t + 1) * ft)
+            ys = []
             for acc, w in ((accg, wg), (accu, wu)):
                 y = jnp.dot(xs[0], w[at[0]:at[0] + SW, fs], preferred_element_type=F32)
                 y = y + jnp.dot(xs[1], w[at[1]:at[1] + SW, fs], preferred_element_type=F32)
-                acc[:, fs] = y + acc[:, fs] if k > 1 else y
-            return carry
-
-        lax.fori_loop(0, FW // ft, step, 0)
-    r = lax.rsqrt(square / D + 1e-5)
-
-    def act(t, carry):
-        fs = pl.ds(pl.multiple_of(t * ft, ft), ft)
-        g = accg[:, fs] * r
-        u = accu[:, fs] * r
-        inner[:, fs] = (g / (1.0 + jnp.exp(-g)) * u).astype(BF)
-        return carry
-
-    lax.fori_loop(0, FW // ft, act, 0)
+                if k:
+                    y = y + acc[:, fs]
+                if last:
+                    ys.append(y * r)
+                else:
+                    acc[:, fs] = y
+            if last:
+                g, u = ys
+                inner[:, fs] = (g / (1.0 + jnp.exp(-g)) * u).astype(BF)
     wcopies[-1].wait()
 
-    HW = CW // 2
+    unit = D // sum(WIDTHS)
+    spans = [(sum(WIDTHS[:i]) * unit, w * unit) for i, w in enumerate(WIDTHS)]
 
     def halves(i):
-        return pl.ds(i * CW, HW), pl.ds(i * CW + HW, HW)
+        at, w = spans[i]
+        return pl.ds(at, w // 2), pl.ds(at + w // 2, w // 2)
 
     copies = {}
 
@@ -710,32 +723,31 @@
         cp.start()
         copies[sem, i] = cp
 
-    ct = tile_of(CW)
-    for i in range(RCHUNKS):
-        for t in range(CW // ct):
-            cs = slice(i * CW + t * ct, i * CW + (t + 1) * ct)
+    for i, (at, w) in enumerate(spans):
+        ct = tile_of(w)
+        for t in range(w // ct):
+            cs = slice(at + t * ct, at + (t + 1) * ct)
             part[:, cs] = jnp.dot(inner[...], wd[:, cs], preferred_element_type=F32).astype(BF)
         ha, hb = halves(i)
         send(i, 0, rows_of(dg), 1, ha, nx)
         send(i, 1, rows_of(dg), 1, hb, ny)
         send(i, 2, rows_of(nx), 0, ha, nx)
         send(i, 3, rows_of(ny), 0, hb, ny)
-    for i in range(RCHUNKS + 1):
-        if i < RCHUNKS:
-            ha, hb = halves(i)
-            for cs, sem, to in ((ha, 0, ny), (hb, 1, nx)):
-                copies[sem, i].wait_recv()
-                rows = rows_of(to)
-                part[rows, cs] = (part[rows, cs].astype(F32) + rs[1, :, cs].astype(F32)).astype(BF)
-                send(i, 4 + sem, rows, 2, cs, to)
-        if i:
-            cs = pl.ds((i - 1) * CW, CW)
-            for sem in (2, 3, 4, 5):
-                copies[sem, i - 1].wait_recv()
-            total = part[my_rows, cs].astype(F32)
-            for place in (0, 2):
-                total = total + rs[place, :, cs].astype(F32)
-            out[:, cs] = (gath[my_rows, cs].astype(F32) + total).astype(BF)
+    for i in range(len(spans)):
+        ha, hb = halves(i)
+        for cs, sem, to in ((ha, 0, ny), (hb, 1, nx)):
+            copies[sem, i].wait_recv()
+            rows = rows_of(to)
+            part[rows, cs] = (part[rows, cs].astype(F32) + rs[1, :, cs].astype(F32)).astype(BF)
+            send(i, 4 + sem, rows, 2, cs, to)
+    for i in range(len(spans)):
+        cs = pl.ds(*spans[i])
+        for sem in (2, 3, 4, 5):
+            copies[sem, i].wait_recv()
+        total = part[my_rows, cs].astype(F32)
+        for place in (0, 2):
+            total = total + rs[place, :, cs].astype(F32)
+        out[:, cs] = (gath[my_rows, cs].astype(F32) + total).astype(BF)
 
     for cps in a_copies:
         for cp in cps:
@@ -785,7 +797,7 @@
             pltpu.VMEM(wg.shape, BF),
             pltpu.VMEM(wu.shape, BF),
             pltpu.VMEM(wd.shape, BF),
-            pltpu.VMEM((G, ratio * R, HEAD_DIM), BF),
+            pltpu.VMEM((R, QW), BF),
             pltpu.VMEM((B, G, 2, R, HEAD_DIM), BF),
             pltpu.VMEM((R, QW), BF),
             pltpu.VMEM((2, R, QW), BF),
@@ -799,14 +811,14 @@
             pltpu.VMEM((R, AW), F32),
             pltpu.VMEM((R, FW), BF),
             dma((3 + 2 * CHUNKS,)),
-            dma((H - 1, G * (2 + ratio))), dma((H - 1, G * (2 + ratio))),
+            dma((H - 1, 2 * G + 1)), dma((H - 1, 2 * G + 1)),
             dma((B, G, 2)), dma((B, G, 2)),
             dma((B, G, 2)), dma((B, G, 2)),
             dma((6,)), dma((6,)),
             dma((G, 2)), dma((G, 2)),
             dma((2, SUBS)), dma((2, SUBS)),
             dma((2, SUBS, 6)), dma((2, SUBS, 6)),
-            dma((6, RCHUNKS)), dma((6, RCHUNKS)),
+            dma((6, len(WIDTHS))), dma((6, len(WIDTHS))),
         ],
         compiler_params=pltpu.CompilerParams(
             collective_id=0, has_side_effects=True, vmem_limit_bytes=67_043_328

time: 97.3 us -> 82.6 us (0.85)
  Pallas kernels: 95.3 us -> 80.4 us
    pallas_call x1, Pallas kernels: 95.3 us -> 80.4 us  [square_call(): pl.pallas_call(functools.partial(square_kernel, H, B), out_shape=jax.Shap...]
where the time goes in v2:
time: 82.6 us; the launch traced here: 82.3 us
  Pallas kernels  80.4 us (97%)
  local copies, waits for them, and re-layouts  1.87 us (2%)
    pallas_call x1, Pallas kernels, square_call(): pl.pallas_call(functools.partial(square_kernel, H, B), out_shape=jax.Shap...  80.4 us
    unnamed x1, local copies, waits for them, and re-layouts  1.87 us

profile of v2, /device:TPU:24, one launch (start us, length us, event | category | flops | bytes accessed | tf_op | source)
XLA Modules:
  0.0 82.3 jit_solution(11422901520933477928)
XLA Ops:
  0.0 80.4 %shard_map.91 = bf16[64,4096]{1,0:T(8,128)(2,1)} custom-call(bf16[64,4096]{1,0:T(8,128)(2,1)} %hid.1, bf16[64,2048]{1,0:T(8,128)(2,1)} %q_in.1, bf16[64,1024]{1,0:T(8,128)(2,1)} %k_in.1, bf16[64,1024]{1,0:T(8,128)(2,1)} %v_in.1, f32[1,4096]{1,0:T(1,128)} %bitcast.1, bf16[512,4096]{1,0:T(8,128)(2,1)} %wo_h.1, bf16[4096,1792]{1,0:T(8,128)(2,1)} %wg_h.1, ...), custom_call_target="tpu_custom_call" | custom-call | tf_op jit(solution)/shard_map/pallas_call | solution.py:790
  80.4 1.9 %copy.11 = bf16[64,4096]{1,0:T(8,128)(2,1)} copy(bf16[64,4096]{1,0:T(8,128)(2,1)} %shard_map.91) | data formatting | bytes 1048576

commit v3 on v2

--- a/solution.py
+++ b/solution.py
@@ -12,9 +12,9 @@
 HEAD_DIM = 128
 CHUNKS = 4
 AHEAD = 2
-SUBS = 4
+SUBS = (2, 2, 2, 2)
 LEAD = 3
-LAG = 3
+LAG = 2
 QB = 128
 WIDTHS = (1, 1, 2, 2, 2)
 LOG2E = 1.4426950408889634
@@ -368,10 +368,10 @@
 
 def square_kernel(
     H, B,
-    hid, q_in, k_in, v_in, gain, wo_h, wg_h, wu_h, wd_h,
+    hid_h, q_h, k_h, v_h, gain, wo_h, wg_h, wu_h, wd_h,
     out,
-    wo, wg, wu, wd, qb, kv, att, attx, hx, sb, rb, part, rs, gath, accg, accu, inner,
-    w_sem, a_s, a_r, z_s, z_r, d_s, d_r, x_s, x_r, at_s, at_r, o_s, o_r, ag_s, ag_r, r2_s, r2_r,
+    hid, q_in, k_in, v_in, wo, wg, wu, wd, qb, kv, att, attx, hx, sb, rb, part, rs, gath, accg, accu, inner,
+    i_sem, w_sem, a_s, a_r, z_s, z_r, d_s, d_r, x_s, x_r, at_s, at_r, o_s, o_r, ag_s, ag_r, r2_s, r2_r,
 ):
     h = lax.axis_index("head")
     b = lax.axis_index("blk")
@@ -388,7 +388,8 @@
     FW = wg.shape[1]
     half = D // 2
     DW = D // 4
-    SW = DW // SUBS
+    grain = DW // sum(SUBS)
+    subs = [(sum(SUBS[:i]) * grain, w * grain) for i, w in enumerate(SUBS)]
 
     ex, ey = h % 2, h // 2
     nx = h + 1 - 2 * ex
@@ -409,6 +410,12 @@
     wcopies.append((wd_h, wd))
     wcopies = [pltpu.make_async_copy(s, d, w_sem.at[n]) for n, (s, d) in enumerate(wcopies)]
 
+    staged = [
+        pltpu.make_async_copy(src, dst, i_sem.at[n])
+        for n, (src, dst) in enumerate(((k_h, k_in), (v_h, v_in), (q_h, q_in), (hid_h, hid)))
+    ]
+    for cp in staged:
+        cp.start()
     barrier = pltpu.get_barrier_semaphore()
     for d in range(1, H):
         pl.semaphore_signal(barrier, inc=1, device_id={"head": lax.rem(h + d, H)}, device_id_type=MESH)
@@ -423,6 +430,9 @@
 
     pl.semaphore_signal(barrier, inc=1, device_id={"blk": partner}, device_id_type=MESH)
     pl.semaphore_wait(barrier, H + jnp.minimum(j, 1) + jnp.minimum(J - 1 - j, 1))
+
+    for cp in staged[:2]:
+        cp.wait()
 
     def rows_of(p):
         return pl.ds(pl.multiple_of(p * T, T), T)
@@ -441,6 +451,8 @@
 
     a_copies = []
     for t, (src, per, n, dst) in enumerate(pieces):
+        if src is q_in:
+            staged[2].wait()
         cps = []
         for d, p in enumerate((dg, nx, ny)):
             cp = remote(src.at[:, piece_cols(p, per, n, dst)], dst, a_s.at[d, t], a_r.at[d, t], "head", p)
@@ -459,6 +471,7 @@
             wo_h.at[:, cs], wo.at[s, pl.ds(QW, QW), core_cols],
             x_s.at[2 + s], x_r.at[2 + s], "head", pair[s],
         ))
+    staged[3].wait()
     for cp in x_copies:
         cp.start()
     share = []
@@ -605,8 +618,8 @@
         share[s].start()
     for s in range(2):
         wcopies[s].wait()
-        for t in range(SUBS):
-            cs = slice(t * SW, (t + 1) * SW)
+        for t in range(0, DW, tile_of(DW)):
+            cs = slice(t, t + tile_of(DW))
             accs[s][:, cs] = jnp.dot(att[...], wo[s, :QW, cs], preferred_element_type=F32)
     for s in range(2):
         share[s].wait_recv()
@@ -614,22 +627,23 @@
         cp.wait_recv()
 
     co = ({"h": nx, "x": h, "y": dg, "d": ny}, {"h": ny, "x": dg, "y": h, "d": nx})
-    order = [(s, i) for i in range(SUBS) for s in range(2)]
+    order = [(s, i) for i in range(len(subs)) for s in range(2)]
     o_copies = {}
     for s, i in order:
-        cs = pl.ds(i * SW, SW)
-        accs[s][:, cs] += jnp.dot(attx[s], wo[s, QW:, i * SW:(i + 1) * SW], preferred_element_type=F32)
+        cs = pl.ds(*subs[i])
+        accs[s][:, cs] += jnp.dot(attx[s], wo[s, QW:, cs], preferred_element_type=F32)
         to = across[s]
         away = (to, co[s]["y" if s == 0 else "x"])
         for n, p in enumerate(away):
-            sb[s, n * T:(n + 1) * T, i * SW:(i + 1) * SW] = accs[s][rows_of(p), cs].astype(BF)
+            sb[s, n * T:(n + 1) * T, cs] = accs[s][rows_of(p), cs].astype(BF)
         cp = remote(sb.at[s, :, cs], rb.at[s, :, cs], o_s.at[s, i], o_r.at[s, i], "head", to)
         cp.start()
         o_copies[s, i] = cp
 
     def cols_of(s, i, other):
         part_index = 1 - mine[s] if other else mine[s]
-        return pl.ds(pl.multiple_of(s * half + part_index * DW + i * SW, SW), SW)
+        at, w = subs[i]
+        return pl.ds(pl.multiple_of(s * half + part_index * DW + at, grain), w)
 
     ag_copies = {}
 
@@ -656,7 +670,7 @@
     for k, (s, i) in enumerate(order):
         o_copies[s, i].wait_recv()
         cs = cols_of(s, i, False)
-        lc = slice(i * SW, (i + 1) * SW)
+        lc = pl.ds(*subs[i])
         gath[my_rows, cs] = (
             hid[:, cs].astype(F32) + (accs[s][my_rows, lc] + rb[s, :T, lc].astype(F32))
         ).astype(BF)
@@ -682,7 +696,8 @@
         s, i = order[k]
         for kind in (1, 2, 4, 5):
             ag_copies[s, i, kind].wait_recv()
-        at = (s * half + i * SW, s * half + DW + i * SW)
+        start, SW = subs[i]
+        at = (s * half + start, s * half + DW + start)
         xs = []
         for a in at:
             x = gath[:, a:a + SW].astype(F32)
@@ -789,10 +804,14 @@
     dma = pltpu.SemaphoreType.DMA
     return pl.pallas_call(
         functools.partial(square_kernel, H, B),
-        out_shape=jax.ShapeDtypeStruct((T, D), BF),
-        in_specs=[vm] * 5 + [hbm] * 4,
+        out_shape=pltpu.VMEM((T, D), BF),
+        in_specs=[hbm] * 4 + [vm] + [hbm] * 4,
         out_specs=vm,
         scratch_shapes=[
+            pltpu.VMEM(hid.shape, BF),
+            pltpu.VMEM(q.shape, BF),
+            pltpu.VMEM(k.shape, BF),
+            pltpu.VMEM(v.shape, BF),
             pltpu.VMEM((2, 2 * QW, D // 4), BF),
             pltpu.VMEM(wg.shape, BF),
             pltpu.VMEM(wu.shape, BF),
@@ -810,18 +829,19 @@
             pltpu.VMEM((R, AW), F32),
             pltpu.VMEM((R, AW), F32),
             pltpu.VMEM((R, FW), BF),
+            dma((4,)),
             dma((3 + 2 * CHUNKS,)),
             dma((H - 1, 2 * G + 1)), dma((H - 1, 2 * G + 1)),
             dma((B, G, 2)), dma((B, G, 2)),
             dma((B, G, 2)), dma((B, G, 2)),
             dma((6,)), dma((6,)),
             dma((G, 2)), dma((G, 2)),
-            dma((2, SUBS)), dma((2, SUBS)),
-            dma((2, SUBS, 6)), dma((2, SUBS, 6)),
+            dma((2, len(SUBS))), dma((2, len(SUBS))),
+            dma((2, len(SUBS), 6)), dma((2, len(SUBS), 6)),
             dma((6, len(WIDTHS))), dma((6, len(WIDTHS))),
         ],
         compiler_params=pltpu.CompilerParams(
-            collective_id=0, has_side_effects=True, vmem_limit_bytes=67_043_328
+            collective_id=0, has_side_effects=True, vmem_limit_bytes=66_400_000
         ),
     )(hid, q, k, v, gain.reshape(1, -1), wo, wg, wu, wd)
 

time: 82.6 us -> 80.2 us (0.971)
  Pallas kernels: 80.4 us -> 79.1 us
  local copies, waits for them, and re-layouts: 1.87 us -> 0.8 us
    pallas_call x1, Pallas kernels: 80.4 us -> 79.1 us  [square_call(): pl.pallas_call(functools.partial(square_kernel, H, B), out_shape=pltpu.VM...]
    unnamed x1, local copies, waits for them, and re-layouts: 1.87 us -> 0.8 us
where the time goes in v3:
time: 80.2 us; the launch traced here: 79.9 us
  Pallas kernels  79.1 us (99%)
    pallas_call x1, Pallas kernels, square_call(): pl.pallas_call(functools.partial(square_kernel, H, B), out_shape=pltpu.VM...  79.1 us

profile of v3, /device:TPU:24, one launch (start us, length us, event | category | flops | bytes accessed | tf_op | source)
XLA Modules:
  0.0 79.9 jit_solution(2807529256535318021)
XLA Ops:
  0.0 79.1 %shard_map.91 = bf16[64,4096]{1,0:T(8,128)(2,1)S(1)} custom-call(bf16[64,4096]{1,0:T(8,128)(2,1)} %hid_h.1, bf16[64,2048]{1,0:T(8,128)(2,1)} %q_h.1, bf16[64,1024]{1,0:T(8,128)(2,1)} %k_h.1, bf16[64,1024]{1,0:T(8,128)(2,1)} %v_h.1, f32[1,4096]{1,0:T(1,128)} %bitcast.1, bf16[512,4096]{1,0:T(8,128)(2,1)} %wo_h.1, bf16[4096,1792]{1,0:T(8,128)(2,1)} %wg_h.1, ...), custom_call_target="tpu_custom_call" | custom-call | tf_op jit(solution)/shard_map/pallas_call | solution.py:805
  79.1 0.8 copy.11

commit v4 on v3

--- a/solution.py
+++ b/solution.py
@@ -368,9 +368,9 @@
 
 def square_kernel(
     H, B,
-    hid_h, q_h, k_h, v_h, gain, wo_h, wg_h, wu_h, wd_h,
+    hid_h, q_h, k_h, v_h, gain_h, wo_h, wg_h, wu_h, wd_h,
     out,
-    hid, q_in, k_in, v_in, wo, wg, wu, wd, qb, kv, att, attx, hx, sb, rb, part, rs, gath, accg, accu, inner,
+    hid, q_in, k_in, v_in, gain, wo, wg, wu, wd, qb, kv, att, attx, hx, sb, rb, part, rs, gath, accg, accu, inner,
     i_sem, w_sem, a_s, a_r, z_s, z_r, d_s, d_r, x_s, x_r, at_s, at_r, o_s, o_r, ag_s, ag_r, r2_s, r2_r,
 ):
     h = lax.axis_index("head")
@@ -412,7 +412,7 @@
 
     staged = [
         pltpu.make_async_copy(src, dst, i_sem.at[n])
-        for n, (src, dst) in enumerate(((k_h, k_in), (v_h, v_in), (q_h, q_in), (hid_h, hid)))
+        for n, (src, dst) in enumerate(((k_h, k_in), (v_h, v_in), (q_h, q_in), (hid_h, hid), (gain_h, gain)))
     ]
     for cp in staged:
         cp.start()
@@ -681,6 +681,7 @@
         if k < LEAD:
             spread_own(s, i)
 
+    staged[4].wait()
     for w in wcopies[2:-1]:
         w.wait()
     ft = tile_of(FW)
@@ -805,13 +806,14 @@
     return pl.pallas_call(
         functools.partial(square_kernel, H, B),
         out_shape=pltpu.VMEM((T, D), BF),
-        in_specs=[hbm] * 4 + [vm] + [hbm] * 4,
+        in_specs=[hbm] * 9,
         out_specs=vm,
         scratch_shapes=[
             pltpu.VMEM(hid.shape, BF),
             pltpu.VMEM(q.shape, BF),
             pltpu.VMEM(k.shape, BF),
             pltpu.VMEM(v.shape, BF),
+            pltpu.VMEM((1, D), F32),
             pltpu.VMEM((2, 2 * QW, D // 4), BF),
             pltpu.VMEM(wg.shape, BF),
             pltpu.VMEM(wu.shape, BF),
@@ -829,7 +831,7 @@
             pltpu.VMEM((R, AW), F32),
             pltpu.VMEM((R, AW), F32),
             pltpu.VMEM((R, FW), BF),
-            dma((4,)),
+            dma((5,)),
             dma((3 + 2 * CHUNKS,)),
             dma((H - 1, 2 * G + 1)), dma((H - 1, 2 * G + 1)),
             dma((B, G, 2)), dma((B, G, 2)),

time: 80.2 us -> 79.4 us (0.990)
  no operation moved by 1% of the time
where the time goes in v4:
time: 79.4 us; the launch traced here: 79.2 us
  Pallas kernels  78.4 us (99%)
  local copies, waits for them, and re-layouts  0.8 us (1%)
    pallas_call x1, Pallas kernels, square_call(): pl.pallas_call(functools.partial(square_kernel, H, B), out_shape=pltpu.VM...  78.4 us

profile of v4, /device:TPU:24, one launch (start us, length us, event | category | flops | bytes accessed | tf_op | source)
XLA Modules:
  0.0 79.2 jit_solution(15096236990001644640)
XLA Ops:
  0.0 78.4 %shard_map.91 = bf16[64,4096]{1,0:T(8,128)(2,1)S(1)} custom-call(bf16[64,4096]{1,0:T(8,128)(2,1)} %hid_h.1, bf16[64,2048]{1,0:T(8,128)(2,1)} %q_h.1, bf16[64,1024]{1,0:T(8,128)(2,1)} %k_h.1, bf16[64,1024]{1,0:T(8,128)(2,1)} %v_h.1, f32[1,4096]{1,0:T(1,128)} %bitcast.1, bf16[512,4096]{1,0:T(8,128)(2,1)} %wo_h.1, bf16[4096,1792]{1,0:T(8,128)(2,1)} %wg_h.1, ...), custom_call_target="tpu_custom_call" | custom-call | tf_op jit(solution)/shard_map/pallas_call | solution.py:806
  78.4 0.8 %copy.11 = bf16[64,4096]{1,0:T(8,128)(2,1)} copy(bf16[64,4096]{1,0:T(8,128)(2,1)S(1)} %shard_map.91) | data formatting | bytes 1048576
